TPU v7x, 32 devices: a whole 2x2x4 slice. The times are simulated.
32 devices in a mesh: rep: 4 (over x, core), fsdp: 8 (over z, y).
Axes of the slice: x: 2, y: 2, z: 4, core: 2. Of those that a mesh axis runs over, the one named last changes fastest.
Arguments:
- tokens: bfloat16 [32768, 1024], P(('rep', 'fsdp')), may hold values from -6 to 6
- cotangent: bfloat16 [32768, 1024], P(('rep', 'fsdp')), may hold values from -6 to 6
- segment_ids: int32 [32, 1024], P(('rep', 'fsdp')), may hold values from 0 to 15, never falling along the last dimension, each value on 1 to 512 neighbouring positions
- attention_weight: float32 [4, 1024, 1024], P(None, 'fsdp'), may hold values from -0.375 to 0.375
- attention_momentum: float32 [4, 1024, 1024], P(None, 'fsdp'), may hold values from -0.1875 to 0.1875
- attention_first: float32 [4, 4, 1024, 1024], P('rep', None, 'fsdp'), may hold values from -112 to 112
- attention_second: float32 [4, 4, 1024, 1024], P('rep', None, 'fsdp'), may hold values from 54.8864 to 876.544
- expand_weight: float32 [1024, 4096], P('fsdp'), may hold values from -0.1875 to 0.1875
- expand_momentum: float32 [1024, 4096], P('fsdp'), may hold values from -0.1875 to 0.1875
- expand_first: float32 [4, 1024, 4096], P('rep', 'fsdp'), may hold values from -128 to 128
- expand_second: float32 [4, 1024, 4096], P('rep', 'fsdp'), may hold values from 85.1968 to 1368.064
- contract_weight: float32 [4096, 1024], P('fsdp'), may hold values from -0.09375 to 0.09375
- contract_momentum: float32 [4096, 1024], P('fsdp'), may hold values from -0.09375 to 0.09375
- contract_first: float32 [4, 4096, 1024], P('rep', 'fsdp'), may hold values from -256 to 256
- contract_second: float32 [4, 4096, 1024], P('rep', 'fsdp'), may hold values from 341.6064 to 5464.064
- vectors: float32 [12, 1024], P(None, 'fsdp'), may hold values from -0.6 to 1.4
- vectors_momentum: float32 [12, 1024], P(None, 'fsdp'), may hold values from -1.25 to 1.25
- vectors_first: float32 [4, 12, 1024], P('rep', None, 'fsdp'), may hold values from -448 to 448
- vectors_second: float32 [4, 12, 1024], P('rep', None, 'fsdp'), may hold values from 876.544 to 14008.32
Outputs:
- layer_output: bfloat16 [32768, 1024], P(('rep', 'fsdp'))
- input_grad: bfloat16 [32768, 1024], P(('rep', 'fsdp'))
- attention_first_new: float32 [4, 4, 1024, 1024], P('rep', None, 'fsdp')
- attention_second_new: float32 [4, 4, 1024, 1024], P('rep', None, 'fsdp')
- outer_attention: float32 [3, 4, 1024, 1024], P(None, None, 'fsdp')
- copy_attention: bfloat16 [4, 1024, 1024], P(None, 'fsdp')
- expand_first_new: float32 [4, 1024, 4096], P('rep', 'fsdp')
- expand_second_new: float32 [4, 1024, 4096], P('rep', 'fsdp')
- outer_expand: float32 [3, 1024, 4096], P(None, 'fsdp')
- copy_expand: bfloat16 [1024, 4096], P('fsdp')
- contract_first_new: float32 [4, 4096, 1024], P('rep', 'fsdp')
- contract_second_new: float32 [4, 4096, 1024], P('rep', 'fsdp')
- outer_contract: float32 [3, 4096, 1024], P(None, 'fsdp')
- copy_contract: bfloat16 [4096, 1024], P('fsdp')
- vectors_first_new: float32 [4, 12, 1024], P('rep', None, 'fsdp')
- vectors_second_new: float32 [4, 12, 1024], P('rep', None, 'fsdp')
- outer_vectors: float32 [3, 12, 1024], P(None, None, 'fsdp')
- copy_vectors: bfloat16 [12, 1024], P(None, 'fsdp')
Inputs may be any that keep to these rules, and one draw needn't show every extreme that they name: `segment_ids`: within a row the numbers never fall; a run of equal numbers is one document, and tokens attend only within their document.
All inputs are finite; a program needn't handle non-finite values.
Results may differ from a plain program's by a relative error of at most 0.012.
The roundings to bfloat16 on the way count: a program that leaves them out, or rounds other values in their place, can miss the bound.
Values may be sent and summed in bfloat16 or wider, within the bound.
A program may use at most 448 MiB of HBM per device.

v0:
```python
from functools import partial
import jax
import jax.numpy as jnp
from jax import lax
from jax.sharding import PartitionSpec as P

D = 1024
H = 16
HD = 64
FF = 4096
LEN = 1024
SEQ_DEV = 1
ADAM_STEP = 4
TOK_DEV = 1024


def norm_forward(values_in, gain_row, shift_row):
    center = values_in - jnp.mean(values_in, axis=-1, keepdims=True)
    inv_scale = lax.rsqrt(jnp.mean(center * center, axis=-1, keepdims=True) + 1e-05)
    normed = center * inv_scale
    return (normed * gain_row + shift_row, normed, inv_scale)


def norm_backward(grad_out, normed, inv_scale, gain_row):
    grad_gain = jnp.sum(grad_out * normed, axis=0)
    grad_shift = jnp.sum(grad_out, axis=0)
    scaled_grad = grad_out * gain_row
    grad_value = inv_scale * (
        scaled_grad
        - jnp.mean(scaled_grad, axis=-1, keepdims=True)
        - normed * jnp.mean(scaled_grad * normed, axis=-1, keepdims=True)
    )
    return (grad_value, grad_gain, grad_shift)


def product_over(left, right):
    return lax.dot_general(
        left, right, (((0,), (0,)), ((), ())), preferred_element_type=jnp.float32
    )


def product_back(left, right):
    return lax.dot_general(
        left, right, (((1,), (1,)), ((), ())), preferred_element_type=jnp.float32
    )


def block_scores(query_block, key_block, row_segments, all_segments):
    scores = jnp.einsum("qhd,khd->hqk", query_block, key_block, preferred_element_type=jnp.float32)
    same_doc = row_segments[:, None] == all_segments[None, :]
    return jnp.where(same_doc[None], scores, -1e30)


def inner_step(weight, gradient, first_moment, second_moment, learn_rate, weight_decay):
    first_new = 0.5 * first_moment + 0.5 * gradient
    second_new = 0.75 * second_moment + 0.25 * gradient * gradient
    update_dir = (
        first_new
        / (1.0 - 0.5**ADAM_STEP)
        / (jnp.sqrt(second_new / (1.0 - 0.75**ADAM_STEP)) + 1e-08)
    )
    return (weight - learn_rate * (update_dir + weight_decay * weight), first_new, second_new)


def per_device(
    tokens,
    cotangent,
    segment_ids,
    attention_weight,
    attention_momentum,
    attention_first,
    attention_second,
    expand_weight,
    expand_momentum,
    expand_first,
    expand_second,
    contract_weight,
    contract_momentum,
    contract_first,
    contract_second,
    vectors,
    vectors_momentum,
    vectors_first,
    vectors_second,
):
    attn_full, vector_full = (
        lax.all_gather(attention_weight.astype(jnp.bfloat16), "fsdp", axis=1, tiled=True),
        lax.all_gather(vectors.astype(jnp.bfloat16), "fsdp", axis=1, tiled=True),
    )
    vector_rows = vector_full.astype(jnp.float32)
    gain_one, gain_two, shift_one, shift_two = (
        vector_rows[0],
        vector_rows[1],
        vector_rows[2],
        vector_rows[3],
    )
    bias_query, bias_value, bias_mixed, bias_down = (
        vector_rows[4],
        vector_rows[5],
        vector_rows[6],
        vector_rows[7],
    )
    bias_up = vector_rows[8:].reshape(FF)
    projected = jnp.einsum("td,nde->nte", tokens, attn_full[:3], preferred_element_type=jnp.float32)
    query_all = ((projected[0] + bias_query) * 0.125).astype(jnp.bfloat16)
    key_all = projected[1].astype(jnp.bfloat16)
    value_all = (projected[2] + bias_value).astype(jnp.bfloat16)
    query_heads = query_all.reshape(SEQ_DEV, LEN, H, HD)
    key_heads = key_all.reshape(SEQ_DEV, LEN, H, HD)
    value_heads = value_all.reshape(SEQ_DEV, LEN, H, HD)
    block_rows = min(512, LEN)
    head_group = min(8, H)
    context_rows = []
    log_sums = []
    seq_index = 0
    for row_start in range(0, LEN, block_rows):
        block_pieces = []
        for head_start in range(0, H, head_group):
            head_part = slice(head_start, head_start + head_group)
            scores = block_scores(
                query_heads[seq_index, row_start : row_start + block_rows, head_part],
                key_heads[seq_index, :, head_part],
                segment_ids[seq_index, row_start : row_start + block_rows],
                segment_ids[seq_index],
            )
            row_max = jnp.max(scores, axis=-1, keepdims=True)
            exp_score = jnp.exp(scores - row_max)
            row_total = jnp.sum(exp_score, axis=-1, keepdims=True)
            probability = (exp_score / row_total).astype(jnp.bfloat16)
            block_pieces.append(
                jnp.einsum(
                    "hqk,khd->qhd",
                    probability,
                    value_heads[seq_index, :, head_part],
                    preferred_element_type=jnp.float32,
                )
            )
            log_sums.append(row_max + jnp.log(row_total))
        context_rows.append(jnp.concatenate(block_pieces, axis=1))
    mixed = jnp.concatenate(context_rows, axis=0).reshape(TOK_DEV, D).astype(jnp.bfloat16)
    attn_out = jnp.dot(mixed, attn_full[3], preferred_element_type=jnp.float32) + bias_mixed
    hidden, normed_one, scale_one = norm_forward(
        tokens.astype(jnp.float32) + attn_out, gain_one, shift_one
    )
    hidden_low = hidden.astype(jnp.bfloat16)
    ffn_expand, ffn_contract = (
        lax.all_gather(expand_weight.astype(jnp.bfloat16), "fsdp", axis=0, tiled=True),
        lax.all_gather(contract_weight.astype(jnp.bfloat16), "fsdp", axis=0, tiled=True),
    )
    pre_act = jnp.dot(hidden_low, ffn_expand, preferred_element_type=jnp.float32) + bias_up
    activated = jax.nn.gelu(pre_act, approximate=False).astype(jnp.bfloat16)
    branch = jnp.dot(activated, ffn_contract, preferred_element_type=jnp.float32) + bias_down
    layer_output, normed_two, scale_two = norm_forward(hidden + branch, gain_two, shift_two)
    grad_sum, grad_gain_two, grad_shift_two = norm_backward(
        cotangent.astype(jnp.float32), normed_two, scale_two, gain_two
    )
    grad_branch = grad_sum.astype(jnp.bfloat16)
    grad_act = product_back(grad_branch, ffn_contract)
    unused_value, gelu_pull = jax.vjp(partial(jax.nn.gelu, approximate=False), pre_act)
    grad_pre_low = gelu_pull(grad_act)[0].astype(jnp.bfloat16)
    grad_hidden = grad_sum + product_back(grad_pre_low, ffn_expand)
    contract_full = product_over(activated, grad_branch)
    expand_full = product_over(hidden_low, grad_pre_low)
    grad_expand, grad_contract = (
        lax.psum_scatter(expand_full, "fsdp", scatter_dimension=0, tiled=True),
        lax.psum_scatter(contract_full, "fsdp", scatter_dimension=0, tiled=True),
    )
    grad_resid, grad_gain_one, grad_shift_one = norm_backward(
        grad_hidden, normed_one, scale_one, gain_one
    )
    grad_attn_out = grad_resid.astype(jnp.bfloat16)
    grad_bias_mixed = jnp.sum(grad_attn_out.astype(jnp.float32), axis=0)
    grad_output_proj = product_over(mixed, grad_attn_out)
    grad_mixed = product_back(grad_attn_out, attn_full[3]).astype(jnp.bfloat16)
    grad_context = grad_mixed.reshape(SEQ_DEV, LEN, H, HD)
    query_grads = []
    lse_index = 0
    seq_index = 0
    key_totals = [
        jnp.zeros((LEN, head_group, HD), jnp.float32) for head_start in range(0, H, head_group)
    ]
    value_totals = [
        jnp.zeros((LEN, head_group, HD), jnp.float32) for head_start in range(0, H, head_group)
    ]
    for row_start in range(0, LEN, block_rows):
        block_pieces = []
        for group_index, head_start in enumerate(range(0, H, head_group)):
            head_part = slice(head_start, head_start + head_group)
            query_block = query_heads[seq_index, row_start : row_start + block_rows, head_part]
            key_block = key_heads[seq_index, :, head_part]
            value_block = value_heads[seq_index, :, head_part]
            ctx_grad = grad_context[seq_index, row_start : row_start + block_rows, head_part]
            scores = block_scores(
                query_block,
                key_block,
                segment_ids[seq_index, row_start : row_start + block_rows],
                segment_ids[seq_index],
            )
            probability = jnp.exp(scores - log_sums[lse_index])
            lse_index = lse_index + 1
            value_totals[group_index] = value_totals[group_index] + jnp.einsum(
                "hqk,qhd->khd",
                probability.astype(jnp.bfloat16),
                ctx_grad,
                preferred_element_type=jnp.float32,
            )
            prob_grad = jnp.einsum(
                "qhd,khd->hqk", ctx_grad, value_block, preferred_element_type=jnp.float32
            )
            row_dot = jnp.sum(probability * prob_grad, axis=-1, keepdims=True)
            score_grad = (probability * (prob_grad - row_dot)).astype(jnp.bfloat16)
            block_pieces.append(
                jnp.einsum(
                    "hqk,khd->qhd", score_grad, key_block, preferred_element_type=jnp.float32
                ).astype(jnp.bfloat16)
            )
            key_totals[group_index] = key_totals[group_index] + jnp.einsum(
                "hqk,qhd->khd", score_grad, query_block, preferred_element_type=jnp.float32
            )
        query_grads.append(jnp.concatenate(block_pieces, axis=1))
    key_grads = jnp.concatenate(
        [key_total.astype(jnp.bfloat16) for key_total in key_totals], axis=1
    )
    value_grads = jnp.concatenate(
        [value_total.astype(jnp.bfloat16) for value_total in value_totals], axis=1
    )
    grad_query = jnp.concatenate(query_grads, axis=0).reshape(TOK_DEV, D) * 0.125
    grad_keys = key_grads.reshape(TOK_DEV, D)
    grad_values = value_grads.reshape(TOK_DEV, D)
    stacked_grads = jnp.stack([grad_query, grad_keys, grad_values])
    grad_qkv = jnp.einsum("td,nte->nde", tokens, stacked_grads, preferred_element_type=jnp.float32)
    input_grad = (
        grad_resid
        + jnp.einsum(
            "nte,nde->td", stacked_grads, attn_full[:3], preferred_element_type=jnp.float32
        )
    ).astype(jnp.bfloat16)
    grad_attention_full = jnp.concatenate([grad_qkv, grad_output_proj[None]], axis=0)
    vector_head = jnp.stack(
        [
            grad_gain_one,
            grad_gain_two,
            grad_shift_one,
            grad_shift_two,
            jnp.sum(grad_query.astype(jnp.float32), axis=0),
            jnp.sum(grad_values.astype(jnp.float32), axis=0),
            grad_bias_mixed,
            jnp.sum(grad_branch.astype(jnp.float32), axis=0),
        ]
    )
    grad_bias_up = jnp.sum(grad_pre_low.astype(jnp.float32), axis=0).reshape(FF // D, D)
    grad_vectors_full = jnp.concatenate([vector_head, grad_bias_up], axis=0)
    grad_attention, grad_vectors = (
        lax.psum_scatter(grad_attention_full, "fsdp", scatter_dimension=1, tiled=True),
        lax.psum_scatter(grad_vectors_full, "fsdp", scatter_dimension=1, tiled=True),
    )
    attention_new = inner_step(
        attention_weight, grad_attention, attention_first[0], attention_second[0], 0.03, 0.1
    )
    expand_new = inner_step(
        expand_weight, grad_expand, expand_first[0], expand_second[0], 0.03, 0.1
    )
    contract_new = inner_step(
        contract_weight, grad_contract, contract_first[0], contract_second[0], 0.015, 0.1
    )
    vectors_new = inner_step(vectors, grad_vectors, vectors_first[0], vectors_second[0], 0.2, 0.0)
    summed = (
        lax.psum((attention_weight - attention_new[0]).astype(jnp.bfloat16), "rep").astype(
            jnp.float32
        ),
        lax.psum((expand_weight - expand_new[0]).astype(jnp.bfloat16), "rep").astype(jnp.float32),
        lax.psum((contract_weight - contract_new[0]).astype(jnp.bfloat16), "rep").astype(
            jnp.float32
        ),
        lax.psum((vectors - vectors_new[0]).astype(jnp.bfloat16), "rep").astype(jnp.float32),
    )
    groups_count = lax.axis_size("rep")
    results = []
    for weight_now, momentum_now, inner_new, diff_total in zip(
        (attention_weight, expand_weight, contract_weight, vectors),
        (attention_momentum, expand_momentum, contract_momentum, vectors_momentum),
        (attention_new, expand_new, contract_new, vectors_new),
        summed,
    ):
        mean_diff = diff_total / groups_count
        momentum_new = 0.5 * momentum_now + mean_diff
        outer_new = weight_now - 0.7 * (mean_diff + 0.5 * momentum_new)
        results.append(
            (
                inner_new[1][None],
                inner_new[2][None],
                jnp.stack([mean_diff, momentum_new, outer_new]),
                outer_new.astype(jnp.bfloat16),
            )
        )
    return (
        layer_output.astype(jnp.bfloat16),
        input_grad,
        results[0][0],
        results[0][1],
        results[0][2],
        results[0][3],
        results[1][0],
        results[1][1],
        results[1][2],
        results[1][3],
        results[2][0],
        results[2][1],
        results[2][2],
        results[2][3],
        results[3][0],
        results[3][1],
        results[3][2],
        results[3][3],
    )


def solution(mesh):
    placed = (
        P(("rep", "fsdp"), None),
        P(("rep", "fsdp"), None),
        P(("rep", "fsdp"), None),
        P(None, "fsdp", None),
        P(None, "fsdp", None),
        P("rep", None, "fsdp", None),
        P("rep", None, "fsdp", None),
        P("fsdp", None),
        P("fsdp", None),
        P("rep", "fsdp", None),
        P("rep", "fsdp", None),
        P("fsdp", None),
        P("fsdp", None),
        P("rep", "fsdp", None),
        P("rep", "fsdp", None),
        P(None, "fsdp"),
        P(None, "fsdp"),
        P("rep", None, "fsdp"),
        P("rep", None, "fsdp"),
    )
    return jax.shard_map(
        per_device,
        mesh=mesh,
        in_specs=placed,
        out_specs=(
            P(("rep", "fsdp"), None),
            P(("rep", "fsdp"), None),
            P("rep", None, "fsdp", None),
            P("rep", None, "fsdp", None),
            P(None, None, "fsdp", None),
            P(None, "fsdp", None),
            P("rep", "fsdp", None),
            P("rep", "fsdp", None),
            P(None, "fsdp", None),
            P("fsdp", None),
            P("rep", "fsdp", None),
            P("rep", "fsdp", None),
            P(None, "fsdp", None),
            P("fsdp", None),
            P("rep", None, "fsdp"),
            P("rep", None, "fsdp"),
            P(None, None, "fsdp"),
            P(None, "fsdp"),
        ),
        check_vma=False,
    )
```

profile of v0, /device:TPU:0, one launch (start us, length us, event | category | flops | bytes accessed | tf_op | source)
XLA Modules:
  0.0 1465.5 jit_solution(9158751748262666368)
XLA Ops:
  16.3 28.9 %all_gather.13 = bf16[12,1024]{1,0:T(8,128)(2,1)S(1)} all-gather(bf16[12,128]{1,0:T(8,128)(2,1)S(1)} %convert_element_type.221), channel_id=1, replica_groups=mesh['rep'=4,'fsdp'=8] {'fsdp'}, dimensions={1}, use_global_device_ids=true | all-gather | bytes 27648 | tf_op jit(solution)/shard_map/all_gather | solution.py:88
  49.2 4.1 copy.37
  54.0 84.8 %all-gather.4.cloned.1.call-done = bf16[4,1024,1024]{1,2,0:T(8,128)(2,1)} async-done(((bf16[4,128,1024]{1,2,0:T(8,128)(2,1)}), bf16[4,1024,1024]{1,2,0:T(8,128)(2,1)}) %all-gather.4.cloned.1.call-update) | async-done | bytes 8388624 | tf_op jit(solution)/shard_map/all_gather | solution.py:87
  138.7 9.0 convolution_bitcast_fusion.1
  147.7 4.6 copy-done.29
  152.7 5.1 fusion.137
  158.2 8.4 select_reduce_fusion.1
  166.6 8.4 select_reduce_fusion.3
  176.6 13.4 fusion.6
  190.0 8.9 fusion.7
  201.7 6.9 fusion.77
  208.6 8.9 fusion.78
  217.6 13.5 fusion.8
  231.1 8.6 fusion.9
  242.1 4.9 fusion.75
  247.1 8.3 fusion.76
  255.6 4.3 fusion.140
  264.1 48.0 %multiply_convert_fusion.4 = (bf16[1024,4096]{1,0:T(8,128)(2,1)}, f32[1024,4096]{1,0:T(8,128)}, f32[1024,4096]{1,0:T(8,128)}) fusion(f32[4096]{0:T(1024)S(1)} %bitcast.308, bf16[1024,4096]{1,0:T(8,128)(2,1)} %all-gather.6.cloned.1.call-done, bf16[1024,1024]{0,1:T(8,128)(2,1)S(1)} %fusion.134.clone.4), kind=kOutput, calls=%fused_computation.17 | convolution fusion | flops 8866758656 | bytes 52445184 | tf_op jit(solution)/shard_map/dot_general | solution.py:150
  312.1 77.4 %all-gather.8.cloned.1.call-done = bf16[4096,1024]{1,0:T(8,128)(2,1)} async-done(((bf16[512,1024]{1,0:T(8,128)(2,1)}), bf16[4096,1024]{1,0:T(8,128)(2,1)}) %all-gather.8.cloned.1.call-update) | async-done | bytes 8388624 | tf_op jit(solution)/shard_map/all_gather | solution.py:148
  389.5 14.9 %fusion.141 = (f32[1024]{0:T(1024)S(1)}, f32[1024,1024]{0,1:T(8,128)S(1)}) fusion(f32[1024]{0:T(1024)S(1)} %bitcast.316, bf16[1024,4096]{1,0:T(8,128)(2,1)} %get-tuple-element.65, bf16[4096,1024]{1,0:T(8,128)(2,1)} %all-gather.8.cloned.1.call-done, f32[1024]{0:T(1024)S(1)} %bitcast.304, f32[1024]{0:T(1024)S(1)} %bitcast.294, ...), kind=kOutput, calls=%fused_computation.264 | convolution fusion | flops 8597273600 | bytes 25190400 | tf_op jit(solution)/shard_map/dot_general | solution.py:152
  410.4 4.3 convert_reduce_fusion.2
  414.7 24.3 %convert_reduce_fusion = (f32[4096]{0:T(1024)}, bf16[1024,4096]{1,0:T(8,128)(2,1)}) fusion(f32[1024,4096]{1,0:T(8,128)} %get-tuple-element.66, f32[1024,4096]{1,0:T(8,128)} %get-tuple-element.120, f32[4096]{0:T(1024)S(1)} %bitcast.309, bf16[1024,1024]{0,1:T(8,128)(2,1)} %get-tuple-element.60, bf16[4096,1024]{1,0:T(8,128)(2,1)} %all-gather.8.cloned.1.call-done), kind=kOutput, calls=%fused_computation.3 | convolution fusion | flops 8661233664 | bytes 52461568 | tf_op jit(solution)/shard_map/dot_general | solution.py:43
  439.0 14.9 %fusion.131 = f32[1024,4096]{1,0:T(8,128)} fusion(bf16[1024,4096]{1,0:T(8,128)(2,1)} %get-tuple-element.58, f32[1024,1024]{0,1:T(8,128)S(1)} %copy-done.7, f32[1024]{0:T(1024)S(1)} %bitcast.305, f32[1024]{0:T(1024)S(1)} %bitcast.295, f32[1024]{0:T(1024)S(1)} %add_rsqrt_fusion.1, f32[1024]{0:T(1024)S(1)} %broadcast_multiply_fusion.5), kind=kOutput, calls=%fused_computation.258 | convolution fusion | flops 8595177472 | bytes 29376512 | tf_op jit(solution)/shard_map/dot_general | solution.py:37
  455.5 19.6 %multiply_reduce_fusion.4 = (f32[1024]{0:T(1024)}, f32[1024]{0:T(1024)S(1)}, f32[1024]{0:T(1024)S(1)}, f32[1024]{0:T(1024)}, f32[1024,1024]{0,1:T(8,128)S(1)}) fusion(f32[1024,1024]{0,1:T(8,128)} %copy-done.6, f32[1024]{0:T(1024)S(1)} %add_rsqrt_fusion.1, f32[1024]{0:T(1024)S(1)} %broadcast_multiply_fusion.5, f32[1024]{0:T(1024)S(1)} %bitcast.296, ...), kind=kOutput, calls=%fused_computation.96 | convolution fusion | flops 8608804864 | bytes 31506432 | tf_op jit(solution)/shard_map/dot_general | solution.py:43
  477.4 5.6 convolution_convert_fusion
  483.0 9.9 fusion.14
  493.0 9.9 fusion.16
  502.9 6.7 fusion.84
  509.7 10.6 fusion.81
  522.0 4.1 copy.44
  526.0 9.4 fusion.95
  535.5 9.3 fusion.96
  544.8 21.2 %multiply_reduce_fusion.3 = (f32[8,512]{1,0:T(8,128)}, f32[8,512]{1,0:T(8,128)}, f32[8,512,1024]{2,1,0:T(8,128)}) fusion(f32[8,512,1024]{2,1,0:T(8,128)} %get-tuple-element.116, f32[8,512]{1,0:T(8,128)} %copy-done.50, pred[512,1024]{1,0:T(8,128)(4,1)S(1)} %copy-done.11, f32[8,512,1024]{2,1,0:T(8,128)} %fusion.96, f32[8,512]{1,0:T(8,128)} %copy-done.52, ...), kind=kOutput, calls=%fused_computation.14 | convolution fusion | flops 570417152 | bytes 69271552 | tf_op jit(solution)/shard_map/qhd,khd->hqk/dot_general | solution.py:207
  566.1 24.3 %multiply_reduce_fusion.1 = (f32[8,512]{1,0:T(8,128)S(1)}, f32[8,512]{1,0:T(8,128)S(1)}, f32[8,512,1024]{2,1,0:T(8,128)}) fusion(f32[8,512,1024]{2,1,0:T(8,128)} %get-tuple-element.113, f32[8,512]{1,0:T(8,128)} %copy-done.54, pred[512,1024]{1,0:T(8,128)(4,1)S(1)} %copy-done.13, f32[8,512,1024]{2,1,0:T(8,128)} %fusion.95, f32[8,512]{1,0:T(8,128)} %copy-done.56, ...), kind=kOutput, calls=%fused_computation.8 | convolution fusion | flops 570417152 | bytes 69271552 | tf_op jit(solution)/shard_map/qhd,khd->hqk/dot_general | solution.py:207
  590.5 52.7 %multiply_convert_fusion.1 = (bf16[8,512,1024]{2,1,0:T(8,128)(2,1)}, bf16[8,512,1024]{2,1,0:T(8,128)(2,1)S(1)}, bf16[8,512,1024]{2,1,0:T(8,128)(2,1)}, bf16[8,512,1024]{2,1,0:T(8,128)(2,1)}) fusion(f32[8,512,1024]{2,1,0:T(8,128)} %get-tuple-element.125, f32[8,512,1024]{2,1,0:T(8,128)} %get-tuple-element.113, f32[8,512]{1,0:T(8,128)S(1)} %get-tuple-element.44, ...), kind=kLoop, calls=%fused_computation.7 | loop fusion | flops 83886080 | bytes 168951808 | tf_op jit(solution)/shard_map/convert_element_type | solution.py:211
  643.2 8.2 fusion.103
  659.9 4.6 copy.43
  664.5 6.0 fusion.89
  670.5 6.2 fusion.90
  676.8 6.3 fusion.88
  695.4 6.9 convolution_bitcast_fusion
  702.3 6.1 pad_maximum_fusion
  710.0 14.9 %fusion.142 = f32[4096,1024]{1,0:T(8,128)} fusion(bf16[1024,4096]{1,0:T(8,128)(2,1)} %get-tuple-element.65, bf16[1024,1024]{0,1:T(8,128)(2,1)S(1)} %copy-done.45), kind=kOutput, calls=%fused_computation.265 | convolution fusion | flops 8589934592 | bytes 27262976 | tf_op jit(solution)/shard_map/dot_general | solution.py:37
  728.3 3.0 copy.47
  731.3 2.9 copy.50
  734.7 3.9 copy.57
  740.4 8.5 fusion.100
  748.9 266.6 %reduce-scatter.5.cloned.1.call-done = f32[4,128,1024]{1,2,0:T(8,128)} async-done(((f32[4,1024,1024]{1,2,0:T(8,128)}), f32[4,128,1024]{1,2,0:T(8,128)}) %reduce-scatter.5.cloned.1.call-update) | async-done | bytes 2097168 | tf_op jit(solution)/shard_map/reduce_scatter | solution.py:254
  1015.5 6.2 fusion.50
  1021.7 276.8 %reduce-scatter.9.cloned.1.call-done = f32[512,1024]{1,0:T(8,128)} async-done(((f32[4096,1024]{1,0:T(8,128)}), f32[512,1024]{1,0:T(8,128)}) %reduce-scatter.9.cloned.1.call-update) | async-done | bytes 2097168 | tf_op jit(solution)/shard_map/reduce_scatter | solution.py:166
  1298.5 7.8 fusion.99
  1306.4 13.0 fusion.47
  1319.4 4.0 copy.58
  1323.4 32.2 %reduce-scatter.11.cloned.1.call-done = f32[12,128]{1,0:T(8,128)} async-done(((f32[12,1024]{1,0:T(8,128)}), f32[12,128]{1,0:T(8,128)}) %reduce-scatter.11.cloned.1.call-update) | async-done | bytes 6160 | tf_op jit(solution)/shard_map/reduce_scatter | solution.py:255
  1357.5 5.9 psum.31
  1364.7 2.9 copy.60
  1367.5 2.9 copy.59
  1370.4 56.4 %all-reduce.3.cloned.1.call-done = (bf16[4,128,1024]{1,2,0:T(8,128)(2,1)}, bf16[128,4096]{1,0:T(8,128)(2,1)}, bf16[512,1024]{1,0:T(8,128)(2,1)}) async-done(((bf16[4,128,1024]{1,2,0:T(8,128)(2,1)}, bf16[128,4096]{1,0:T(8,128)(2,1)}, bf16[512,1024]{1,0:T(8,128)(2,1)}), (bf16[4,128,1024]{1,2,0:T(8,128)(2,1)}, bf16[128,4096]{1,0:T(8,128)(2,1)}, bf16[512,1024]{1,0:T(8,128)(2,1)})) %all-reduce.3.cloned.1.call-update) | async-done | bytes 3145744 | tf_op jit(solution)/shard_map/psum | solution.py:268
  1426.8 5.0 fusion.125
  1433.1 6.0 pad_maximum_fusion.2
  1439.1 6.7 copy.61
  1445.8 3.6 fusion.127
  1451.7 3.1 pad_maximum_fusion.3
  1454.8 3.3 pad_maximum_fusion.4
  (297 shorter events, 71.4 us)
Async XLA Ops:
  7.2 131.6 %all-gather.4.cloned.1.call-start = ((), (), s32[]{:S(2)}) async-start(), calls=%async_computation.4 | async-start | bytes 9437184 | tf_op jit(solution)/shard_map/all_gather | solution.py:87
  10.5 35.4 %copy-start.84 = (s32[1,1024]{1,0:T(1,128)S(1)}, s32[1,1024]{1,0:T(1,128)}, u32[]{:S(2)}) copy-start(s32[1,1024]{1,0:T(1,128)} %param.21) | copy-start | bytes 12292
  10.5 253.7 %all-gather.6.cloned.1.call-start = ((), (), s32[]{:S(2)}) async-start(), calls=%async_computation.5 | async-start | bytes 9437184 | tf_op jit(solution)/shard_map/all_gather | solution.py:147
  13.3 376.3 %all-gather.8.cloned.1.call-start = ((), (), s32[]{:S(2)}) async-start(), calls=%async_computation.6 | async-start | bytes 9437184 | tf_op jit(solution)/shard_map/all_gather | solution.py:148
  13.3 33.4 %copy-start.36 = (bf16[1024,1024]{1,0:T(8,128)(2,1)S(1)}, bf16[1024,1024]{1,0:T(8,128)(2,1)}, u32[]{:S(2)}) copy-start(bf16[1024,1024]{1,0:T(8,128)(2,1)} %param.20) | copy-start | bytes 6291460
  16.2 724.2 %reduce-scatter.7.cloned.1.call-start = ((), (), s32[]{:S(2)}) async-start(), calls=%async_computation.8 | async-start | bytes 18874368 | tf_op jit(solution)/shard_map/reduce_scatter | solution.py:165
  49.2 89.5 %copy-start.37 = (bf16[1024,1024]{1,0:T(8,128)(2,1)S(1)}, bf16[1024,1024]{1,0:T(8,128)(2,1)}, u32[]{:S(2)}) copy-start(bf16[1024,1024]{1,0:T(8,128)(2,1)} %param.19) | copy-start | bytes 6291460
  54.0 154.6 %copy-start.10 = (pred[512,1024]{1,0:T(8,128)(4,1)}, pred[512,1024]{1,0:T(8,128)(4,1)S(1)}, u32[]{:S(2)}) copy-start(pred[512,1024]{1,0:T(8,128)(4,1)S(1)} %get-tuple-element.108) | copy-start | bytes 1572868
  54.0 193.1 %copy-start.12 = (pred[512,1024]{1,0:T(8,128)(4,1)}, pred[512,1024]{1,0:T(8,128)(4,1)S(1)}, u32[]{:S(2)}) copy-start(pred[512,1024]{1,0:T(8,128)(4,1)S(1)} %get-tuple-element.109) | copy-start | bytes 1572868
  152.7 64.9 %copy-start.4 = (bf16[1,1024,1024]{1,2,0:T(8,128)(2,1)}, bf16[1,1024,1024]{1,2,0:T(8,128)(2,1)S(1)}, u32[]{:S(2)}) copy-start(bf16[1,1024,1024]{1,2,0:T(8,128)(2,1)S(1)} %slice.220) | copy-start | bytes 6291460
  158.2 59.4 %copy-start.16 = (bf16[1,1024,16,64]{1,3,2,0:T(8,128)(2,1)}, bf16[1,1024,16,64]{1,3,2,0:T(8,128)(2,1)S(1)}, u32[]{:S(2)}) copy-start(bf16[1,1024,16,64]{1,3,2,0:T(8,128)(2,1)S(1)} %multiply_convert_fusion.5) | copy-start | bytes 6291460
  166.6 80.5 %copy-start.58 = (f32[8,512]{1,0:T(8,128)}, f32[8,512]{1,0:T(8,128)S(1)}, u32[]{:S(2)}) copy-start(f32[8,512]{1,0:T(8,128)S(1)} %get-tuple-element.112) | copy-start | bytes 49156
  175.0 33.6 %copy-start.60 = (f32[8,512]{1,0:T(8,128)}, f32[8,512]{1,0:T(8,128)S(1)}, u32[]{:S(2)}) copy-start(f32[8,512]{1,0:T(8,128)S(1)} %get-tuple-element.115) | copy-start | bytes 49156
  190.0 8.9 copy-start.62
  190.0 18.6 %copy-start.70 = (f32[8,512]{1,0:T(8,128)}, f32[8,512]{1,0:T(8,128)S(1)}, u32[]{:S(2)}) copy-start(f32[8,512]{1,0:T(8,128)S(1)} %get-tuple-element.48) | copy-start | bytes 49156
  190.0 11.7 copy-start
  217.6 22.1 %copy-start.18 = (bf16[1,1024,16,64]{1,3,2,0:T(8,128)(2,1)S(1)}, bf16[1,1024,16,64]{1,3,2,0:T(8,128)(2,1)}, u32[]{:S(2)}) copy-start(bf16[1,1024,16,64]{1,3,2,0:T(8,128)(2,1)} %add_convert_fusion.2) | copy-start | bytes 6291460
  231.1 16.0 %copy-start.72 = (f32[8,512]{1,0:T(8,128)}, f32[8,512]{1,0:T(8,128)S(1)}, u32[]{:S(2)}) copy-start(f32[8,512]{1,0:T(8,128)S(1)} %get-tuple-element.50) | copy-start | bytes 49156
  231.1 11.0 copy-start.1
  264.1 125.4 %copy-start.94 = (f32[1,1024]{1,0:T(1,128)S(1)}, f32[1,1024]{1,0:T(1,128)}, u32[]{:S(2)}) copy-start(f32[1,1024]{1,0:T(1,128)} %get-tuple-element.99) | copy-start | bytes 12292
  414.7 24.3 %copy-start.7 = (f32[1024,1024]{0,1:T(8,128)S(1)}, f32[1024,1024]{0,1:T(8,128)}, u32[]{:S(2)}) copy-start(f32[1024,1024]{0,1:T(8,128)} %copy-done.6) | copy-start | bytes 12582916
  454.0 21.2 %copy-start.61 = (f32[8,512]{1,0:T(8,128)S(1)}, f32[8,512]{1,0:T(8,128)}, u32[]{:S(2)}) copy-start(f32[8,512]{1,0:T(8,128)} %copy-done.60) | copy-start | bytes 49156
  454.0 21.2 %copy-start.71 = (f32[8,512]{1,0:T(8,128)S(1)}, f32[8,512]{1,0:T(8,128)}, u32[]{:S(2)}) copy-start(f32[8,512]{1,0:T(8,128)} %copy-done.70) | copy-start | bytes 49156
  454.0 21.2 %copy-start.63 = (f32[8,512]{1,0:T(8,128)S(1)}, f32[8,512]{1,0:T(8,128)}, u32[]{:S(2)}) copy-start(f32[8,512]{1,0:T(8,128)} %copy-done.62) | copy-start | bytes 49156
  454.0 21.2 %copy-start.75 = (f32[8,512]{1,0:T(8,128)S(1)}, f32[8,512]{1,0:T(8,128)}, u32[]{:S(2)}) copy-start(f32[8,512]{1,0:T(8,128)} %copy-done.74) | copy-start | bytes 49156
  454.0 21.2 %copy-start.59 = (f32[8,512]{1,0:T(8,128)S(1)}, f32[8,512]{1,0:T(8,128)}, u32[]{:S(2)}) copy-start(f32[8,512]{1,0:T(8,128)} %copy-done.58) | copy-start | bytes 49156
  454.0 21.2 %copy-start.73 = (f32[8,512]{1,0:T(8,128)S(1)}, f32[8,512]{1,0:T(8,128)}, u32[]{:S(2)}) copy-start(f32[8,512]{1,0:T(8,128)} %copy-done.72) | copy-start | bytes 49156
  454.0 21.3 %copy-start.65 = (f32[8,512]{1,0:T(8,128)S(1)}, f32[8,512]{1,0:T(8,128)}, u32[]{:S(2)}) copy-start(f32[8,512]{1,0:T(8,128)} %copy-done.64) | copy-start | bytes 49156
  454.0 21.3 %copy-start.77 = (f32[8,512]{1,0:T(8,128)S(1)}, f32[8,512]{1,0:T(8,128)}, u32[]{:S(2)}) copy-start(f32[8,512]{1,0:T(8,128)} %copy-done.76) | copy-start | bytes 49156
  454.0 561.5 %reduce-scatter.5.cloned.1.call-start = ((), (), s32[]{:S(2)}) async-start(), calls=%async_computation.7 | async-start | bytes 18874368 | tf_op jit(solution)/shard_map/reduce_scatter | solution.py:254
  455.5 19.8 %copy-start.8 = (f32[1024,1024]{0,1:T(8,128)S(1)}, f32[1024,1024]{0,1:T(8,128)}, u32[]{:S(2)}) copy-start(f32[1024,1024]{0,1:T(8,128)} %copy-done.6) | copy-start | bytes 12582916
  475.2 34.4 %copy-start.50 = (f32[8,512]{1,0:T(8,128)}, f32[8,512]{1,0:T(8,128)S(1)}, u32[]{:S(2)}) copy-start(f32[8,512]{1,0:T(8,128)S(1)} %log_add_fusion.3) | copy-start | bytes 49156
  475.3 27.6 %copy-start.52 = (f32[8,512]{1,0:T(8,128)}, f32[8,512]{1,0:T(8,128)S(1)}, u32[]{:S(2)}) copy-start(f32[8,512]{1,0:T(8,128)S(1)} %log_add_fusion.2) | copy-start | bytes 49156
  475.3 17.7 %copy-start.54 = (f32[8,512]{1,0:T(8,128)}, f32[8,512]{1,0:T(8,128)S(1)}, u32[]{:S(2)}) copy-start(f32[8,512]{1,0:T(8,128)S(1)} %log_add_fusion.1) | copy-start | bytes 49156
  483.0 10.0 copy-start.30
  483.0 19.9 %slice-start = ((s8[16777216]{0:T(1024)(128)(4,1)}), s8[4194304]{0:T(1024)(128)(4,1)S(1)}, s32[]{:S(2)}) async-start(s8[16777216]{0:T(1024)(128)(4,1)} %bitcast.261), calls=%async_computation.12 | async-start | bytes 8388608
  483.0 19.9 %slice-start.1 = ((s8[16777216]{0:T(1024)(128)(4,1)}), s8[4194304]{0:T(1024)(128)(4,1)S(1)}, s32[]{:S(2)}) async-start(s8[16777216]{0:T(1024)(128)(4,1)} %bitcast.261), calls=%async_computation.13 | async-start | bytes 8388608
  493.0 9.9 slice-start.2
  493.0 9.9 slice-start.3
  493.0 9.9 copy-start.11
  509.7 10.6 copy-start.25
  526.0 9.5 copy-start.20
  526.0 18.8 %slice-start.4 = ((s8[16777216]{0:T(1024)(128)(4,1)}), s8[4194304]{0:T(1024)(128)(4,1)S(1)}, s32[]{:S(2)}) async-start(s8[16777216]{0:T(1024)(128)(4,1)} %bitcast.263), calls=%async_computation.16 | async-start | bytes 8388608
  526.0 18.8 %slice-start.5 = ((s8[16777216]{0:T(1024)(128)(4,1)}), s8[4194304]{0:T(1024)(128)(4,1)S(1)}, s32[]{:S(2)}) async-start(s8[16777216]{0:T(1024)(128)(4,1)} %bitcast.263), calls=%async_computation.17 | async-start | bytes 8388608
  535.5 9.4 slice-start.6
  535.5 9.4 slice-start.7
  566.1 24.4 %copy-start.51 = (f32[8,512]{1,0:T(8,128)S(1)}, f32[8,512]{1,0:T(8,128)}, u32[]{:S(2)}) copy-start(f32[8,512]{1,0:T(8,128)} %copy-done.50) | copy-start | bytes 49156
  566.1 24.4 %copy-start.53 = (f32[8,512]{1,0:T(8,128)S(1)}, f32[8,512]{1,0:T(8,128)}, u32[]{:S(2)}) copy-start(f32[8,512]{1,0:T(8,128)} %copy-done.52) | copy-start | bytes 49156
  566.1 24.4 %copy-start.55 = (f32[8,512]{1,0:T(8,128)S(1)}, f32[8,512]{1,0:T(8,128)}, u32[]{:S(2)}) copy-start(f32[8,512]{1,0:T(8,128)} %copy-done.54) | copy-start | bytes 49156
  566.1 24.4 %copy-start.57 = (f32[8,512]{1,0:T(8,128)S(1)}, f32[8,512]{1,0:T(8,128)}, u32[]{:S(2)}) copy-start(f32[8,512]{1,0:T(8,128)} %copy-done.56) | copy-start | bytes 49156
  566.1 24.4 %copy-start.68 = (f32[8,512]{1,0:T(8,128)S(1)}, f32[8,512]{1,0:T(8,128)}, u32[]{:S(2)}) copy-start(f32[8,512]{1,0:T(8,128)} %get-tuple-element.46) | copy-start | bytes 49156
  566.1 24.4 %copy-start.69 = (f32[8,512]{1,0:T(8,128)S(1)}, f32[8,512]{1,0:T(8,128)}, u32[]{:S(2)}) copy-start(f32[8,512]{1,0:T(8,128)} %get-tuple-element.47) | copy-start | bytes 49156
  643.2 11.3 copy-start.2
  643.2 9.1 copy-start.3
  643.2 9.7 copy-start.17
  670.5 12.5 slice-start.10
  708.5 590.0 %reduce-scatter.9.cloned.1.call-start = ((), (), s32[]{:S(2)}) async-start(), calls=%async_computation.9 | async-start | bytes 18874368 | tf_op jit(solution)/shard_map/reduce_scatter | solution.py:166
  724.9 630.6 %reduce-scatter.11.cloned.1.call-start = ((), (), s32[]{:S(2)}) async-start(), calls=%async_computation.10 | async-start | bytes 73728 | tf_op jit(solution)/shard_map/reduce_scatter | solution.py:255
  740.1 275.4 %copy-start.15 = (f32[4,128,1024]{1,2,0:T(8,128)S(1)}, f32[4,128,1024]{1,2,0:T(8,128)}, u32[]{:S(2)}) copy-start(f32[4,128,1024]{1,2,0:T(8,128)} %copy-done.14) | copy-start | bytes 6291460
  740.1 686.7 %all-reduce.3.cloned.1.call-start = ((), (), s32[]{:S(2)}) async-start(), calls=%async_computation.11 | async-start | bytes 6291456 | tf_op jit(solution)/shard_map/psum | solution.py:268
  1319.4 36.2 %copy-start.67 = (f32[12,128]{1,0:T(8,128)S(1)}, f32[12,128]{1,0:T(8,128)}, u32[]{:S(2)}) copy-start(f32[12,128]{1,0:T(8,128)} %param.34) | copy-start | bytes 18436
  1319.4 36.2 %copy-start.90 = (f32[1,12,128]{2,0,1:T(1,128)S(1)}, f32[1,12,128]{2,0,1:T(1,128)}, u32[]{:S(2)}) copy-start(f32[1,12,128]{2,0,1:T(1,128)} %param.36) | copy-start | bytes 18436
  1319.4 36.2 %copy-start.91 = (f32[1,12,128]{2,0,1:T(1,128)S(1)}, f32[1,12,128]{2,0,1:T(1,128)}, u32[]{:S(2)}) copy-start(f32[1,12,128]{2,0,1:T(1,128)} %param.37) | copy-start | bytes 18436
  1319.4 44.0 %copy-start.89 = (f32[12,128]{1,0:T(8,128)S(1)}, f32[12,128]{1,0:T(8,128)}, u32[]{:S(2)}) copy-start(f32[12,128]{1,0:T(8,128)} %param.35) | copy-start | bytes 18436
  (52 other events, 237.5 us)
Sparse Core Ops, SparseCore 0:
  10.6 128.0 all-gather.3
  141.4 122.6 all-gather.5
  266.8 122.6 all-gather.7
  454.1 278.3 reduce-scatter.6
  736.1 279.3 reduce-scatter.4
  1019.1 279.3 reduce-scatter.8
  1301.6 53.9 reduce-scatter.10
  1359.3 67.5 all-reduce.2
where the time goes:
time: 1480 us; the launch traced here: 1470 us
  waiting for transfers between devices  796 us (54%)
  matrix products  386 us (26%)
  other arithmetic  150 us (10%)
  local copies, waits for them, and re-layouts  82.1 us (6%)
  blocking collectives  34.9 us (2%)
  between operations  16 us (1%)
    reduce_scatter x1, waiting for transfers between devices, per_device(): lax.psum_scatter(contract_full, 'fsdp', scatter_dimension=0, tiled=True)  277 us
    reduce_scatter x1, waiting for transfers between devices, per_device(): lax.psum_scatter(grad_attention_full, 'fsdp', scatter_dimension=1, tiled=...  267 us
    all_gather x1, waiting for transfers between devices, per_device(): lax.all_gather(attention_weight.astype(jnp.bfloat16), 'fsdp', axis=1, til...  84.8 us
    all_gather x1, waiting for transfers between devices, per_device(): lax.all_gather(contract_weight.astype(jnp.bfloat16), 'fsdp', axis=0, tile...  77.4 us
    dot_general x4, matrix products, per_device(): jnp.einsum('qhd,khd->hqk', ctx_grad, value_block, preferred_element_type=...  64.3 us
    unnamed x230, local copies, waits for them, and re-layouts  62 us
    psum x1, waiting for transfers between devices, per_device(): lax.psum((attention_weight - attention_new[0]).astype(jnp.bfloat16), 'rep')  56.4 us
    convert_element_type x1, other arithmetic, per_device(): score_grad = (probability * (prob_grad - row_dot)).astype(jnp.bfloat16)  52.7 us
  transfers between devices with their start and end apart: 8, of which 7 were waited for; matrix products, arithmetic and copies ran while one was open for 34% of the time, Pallas kernels for 0%

commit v1 on v0

--- a/solution.py
+++ b/solution.py
@@ -12,6 +12,27 @@
 SEQ_DEV = 1
 ADAM_STEP = 4
 TOK_DEV = 1024
+
+
+def ring_gather(value, axis, dim):
+    length, index, span = (lax.axis_size(axis), lax.axis_index(axis), value.shape[dim])
+    upward = [(i, (i + 1) % length) for i in range(length)]
+    left = [(i, (i - 1) % length) for i in range(length)]
+    out = jnp.zeros((*value.shape[:dim], length * span, *value.shape[dim + 1 :]), value.dtype)
+    out = lax.dynamic_update_slice_in_dim(out, value, index * span, axis=dim)
+    from_left = from_right = value
+    half = length // 2
+    for step in range(1, half + 1):
+        from_left = lax.ppermute(from_left, axis, upward)
+        out = lax.dynamic_update_slice_in_dim(
+            out, from_left, (index - step) % length * span, axis=dim
+        )
+        if step < length - half:
+            from_right = lax.ppermute(from_right, axis, left)
+            out = lax.dynamic_update_slice_in_dim(
+                out, from_right, (index + step) % length * span, axis=dim
+            )
+    return out
 
 
 def norm_forward(values_in, gain_row, shift_row):
@@ -84,7 +105,7 @@
     vectors_second,
 ):
     attn_full, vector_full = (
-        lax.all_gather(attention_weight.astype(jnp.bfloat16), "fsdp", axis=1, tiled=True),
+        ring_gather(attention_weight.astype(jnp.bfloat16), "fsdp", 1),
         lax.all_gather(vectors.astype(jnp.bfloat16), "fsdp", axis=1, tiled=True),
     )
     vector_rows = vector_full.astype(jnp.float32)

time: 1480 us -> 1520 us (1.027)
  blocking collectives: 34.9 us -> 70.4 us
  waiting for transfers between devices: 796 us -> 775 us
  starting transfers between devices: 0.58 us -> 20.1 us
  local copies, waits for them, and re-layouts: 82.1 us -> 97.9 us
    ppermute x0 -> x7, waiting for transfers between devices: none -> 143 us  [the longest x4 127 us: ring_gather(): from_left = lax.ppermute(from_left, axis, upward)]
    all_gather x1 -> x0, waiting for transfers between devices: 84.8 us -> none  [per_device(): lax.all_gather(attention_weight.astype(jnp.bfloat16), 'fsdp', axis=1, til...]
    all_gather x1, waiting for transfers between devices: 77.4 us -> 0.01 us  [per_device(): lax.all_gather(contract_weight.astype(jnp.bfloat16), 'fsdp', axis=0, tile...]
    all_gather x1, blocking collectives: 28.9 us -> 64.6 us  [per_device(): lax.all_gather(vectors.astype(jnp.bfloat16), 'fsdp', axis=1, tiled=True)]
    ppermute x0 -> x7, starting transfers between devices: none -> 19.4 us  [the longest x3 10.6 us: ring_gather(): from_right = lax.ppermute(from_right, axis, left)]
    unnamed x230 -> x236, local copies, waits for them, and re-layouts: 62 us -> 62.5 us
  transfers between devices with their start and end apart: 8 -> 14, of which waited for: 7 -> 8; matrix products, arithmetic and copies ran while one was open for 34% -> 34% of each run, Pallas kernels for 0% -> 0%
where the time goes in v1:
time: 1520 us
  waiting for transfers between devices  775 us (51%)
  matrix products  390 us (26%)
  other arithmetic  148 us (10%)
  local copies, waits for them, and re-layouts  97.9 us (6%)
  blocking collectives  70.4 us (5%)
  starting transfers between devices  20.1 us (1%)
  between operations  15.7 us (1%)
    reduce_scatter x1, waiting for transfers between devices, per_device(): lax.psum_scatter(contract_full, 'fsdp', scatter_dimension=0, tiled=True)  277 us
    reduce_scatter x1, waiting for transfers between devices, per_device(): lax.psum_scatter(grad_attention_full, 'fsdp', scatter_dimension=1, tiled=...  266 us
    ppermute x4, waiting for transfers between devices, ring_gather(): from_left = lax.ppermute(from_left, axis, upward)  127 us
    all_gather x1, blocking collectives, per_device(): lax.all_gather(vectors.astype(jnp.bfloat16), 'fsdp', axis=1, tiled=True)  64.6 us
    dot_general x4, matrix products, per_device(): jnp.einsum('qhd,khd->hqk', ctx_grad, value_block, preferred_element_type=...  64.3 us
    unnamed x236, local copies, waits for them, and re-layouts  62.5 us
    psum x1, waiting for transfers between devices, per_device(): lax.psum((attention_weight - attention_new[0]).astype(jnp.bfloat16), 'rep')  56.5 us
    convert_element_type x1, other arithmetic, per_device(): score_grad = (probability * (prob_grad - row_dot)).astype(jnp.bfloat16)  52.8 us
  transfers between devices with their start and end apart: 14, of which 8 were waited for; matrix products, arithmetic and copies ran while one was open for 34% of the time, Pallas kernels for 0%

profile of v1, /device:TPU:0, one launch (start us, length us, event | category | flops | bytes accessed | tf_op | source)
XLA Modules:
  0.0 1516.4 jit_solution(11535919195929365812)
XLA Ops:
  23.1 53.1 %collective-permute-done = bf16[4,128,1024]{1,2,0:T(8,128)(2,1)S(1)} collective-permute-done((bf16[4,128,1024]{1,2,0:T(8,128)(2,1)S(1)}, bf16[4,128,1024]{1,2,0:T(8,128)(2,1)S(1)}, u32[]{:S(2)}, u32[]{:S(2)}) %collective-permute-start) | collective-permute-done | bytes 1048608 | tf_op jit(solution)/shard_map/ppermute | solution.py:26
  78.7 4.0 collective-permute-start.3
  82.7 60.0 %collective-permute-done.2 = bf16[4,128,1024]{1,2,0:T(8,128)(2,1)} collective-permute-done((bf16[4,128,1024]{1,2,0:T(8,128)(2,1)S(1)}, bf16[4,128,1024]{1,2,0:T(8,128)(2,1)}, u32[]{:S(2)}, u32[]{:S(2)}) %collective-permute-start.2) | collective-permute-done | bytes 1048608 | tf_op jit(solution)/shard_map/ppermute | solution.py:26
  147.0 64.6 %all_gather.9 = bf16[12,1024]{1,0:T(8,128)(2,1)S(1)} all-gather(bf16[12,128]{1,0:T(8,128)(2,1)S(1)} %convert_element_type.221), channel_id=1, replica_groups=mesh['rep'=4,'fsdp'=8] {'fsdp'}, dimensions={1}, use_global_device_ids=true | all-gather | bytes 27648 | tf_op jit(solution)/shard_map/all_gather | solution.py:109
  212.3 3.5 collective-permute-start.5
  219.1 4.0 copy.37
  234.8 15.5 %collective-permute-done.5 = bf16[4,128,1024]{1,2,0:T(8,128)(2,1)} collective-permute-done((bf16[4,128,1024]{1,2,0:T(8,128)(2,1)}, bf16[4,128,1024]{1,2,0:T(8,128)(2,1)}, u32[]{:S(2)}, u32[]{:S(2)}) %collective-permute-start.5) | collective-permute-done | bytes 1048608 | tf_op jit(solution)/shard_map/ppermute | solution.py:31
  252.8 14.1 collective-permute-done.6
  268.0 9.0 convolution_bitcast_fusion.1
  277.0 4.6 copy-done.30
  281.9 5.1 fusion.137
  287.4 9.2 select_reduce_fusion.1
  296.6 8.4 select_reduce_fusion.3
  306.6 13.8 fusion.6
  320.4 8.1 fusion.7
  331.1 6.9 fusion.77
  338.0 9.3 fusion.78
  347.3 13.5 fusion.8
  360.7 8.3 fusion.9
  371.3 4.9 fusion.75
  376.4 8.3 fusion.76
  384.9 4.3 fusion.140
  391.9 48.2 %multiply_convert_fusion.4 = (bf16[1024,4096]{1,0:T(8,128)(2,1)}, f32[1024,4096]{1,0:T(8,128)}, f32[1024,4096]{1,0:T(8,128)}) fusion(f32[4096]{0:T(1024)S(1)} %bitcast.308, bf16[1024,4096]{1,0:T(8,128)(2,1)} %all-gather.3.cloned.1.call-done, bf16[1024,1024]{0,1:T(8,128)(2,1)S(1)} %fusion.134.clone.4), kind=kOutput, calls=%fused_computation.17 | convolution fusion | flops 8866758656 | bytes 52445184 | tf_op jit(solution)/shard_map/dot_general | solution.py:171
  440.1 14.9 fusion.141
  461.0 4.5 convert_reduce_fusion.2
  465.4 24.3 %convert_reduce_fusion = (f32[4096]{0:T(1024)}, bf16[1024,4096]{1,0:T(8,128)(2,1)}) fusion(f32[1024,4096]{1,0:T(8,128)} %get-tuple-element.66, f32[1024,4096]{1,0:T(8,128)} %get-tuple-element.122, f32[4096]{0:T(1024)S(1)} %bitcast.309, bf16[1024,1024]{0,1:T(8,128)(2,1)} %get-tuple-element.60, bf16[4096,1024]{1,0:T(8,128)(2,1)} %all-gather.5.cloned.1.call-done), kind=kOutput, calls=%fused_computation.3 | convolution fusion | flops 8661233664 | bytes 52461568 | tf_op jit(solution)/shard_map/dot_general | solution.py:64
  489.8 14.9 fusion.131
  509.2 18.2 %multiply_reduce_fusion.4 = (f32[1024]{0:T(1024)}, f32[1024]{0:T(1024)S(1)}, f32[1024]{0:T(1024)S(1)}, f32[1024]{0:T(1024)}, f32[1024,1024]{0,1:T(8,128)S(1)}) fusion(f32[1024,1024]{0,1:T(8,128)S(1)} %copy-done.8, f32[1024]{0:T(1024)S(1)} %add_rsqrt_fusion.1, f32[1024]{0:T(1024)S(1)} %broadcast_multiply_fusion.5, f32[1024]{0:T(1024)S(1)} %bitcast.296, ...), kind=kOutput, calls=%fused_computation.96 | convolution fusion | flops 8608804864 | bytes 31506432 | tf_op jit(solution)/shard_map/dot_general | solution.py:64
  529.4 5.6 convolution_convert_fusion
  535.1 10.1 fusion.14
  545.2 9.9 fusion.16
  555.2 6.7 fusion.84
  561.9 10.6 fusion.81
  574.2 4.2 copy.44
  578.4 9.4 fusion.95
  587.9 9.3 fusion.96
  597.2 21.2 %multiply_reduce_fusion.3 = (f32[8,512]{1,0:T(8,128)}, f32[8,512]{1,0:T(8,128)}, f32[8,512,1024]{2,1,0:T(8,128)}) fusion(f32[8,512,1024]{2,1,0:T(8,128)} %get-tuple-element.118, f32[8,512]{1,0:T(8,128)} %copy-done.53, pred[512,1024]{1,0:T(8,128)(4,1)S(1)} %copy-done.11, f32[8,512,1024]{2,1,0:T(8,128)} %fusion.96, f32[8,512]{1,0:T(8,128)} %copy-done.55, ...), kind=kOutput, calls=%fused_computation.14 | convolution fusion | flops 570417152 | bytes 69271552 | tf_op jit(solution)/shard_map/qhd,khd->hqk/dot_general | solution.py:228
  618.4 24.4 %multiply_reduce_fusion.1 = (f32[8,512]{1,0:T(8,128)S(1)}, f32[8,512]{1,0:T(8,128)S(1)}, f32[8,512,1024]{2,1,0:T(8,128)}) fusion(f32[8,512,1024]{2,1,0:T(8,128)} %get-tuple-element.115, f32[8,512]{1,0:T(8,128)} %copy-done.57, pred[512,1024]{1,0:T(8,128)(4,1)S(1)} %copy-done.13, f32[8,512,1024]{2,1,0:T(8,128)} %fusion.95, f32[8,512]{1,0:T(8,128)} %copy-done.59, ...), kind=kOutput, calls=%fused_computation.8 | convolution fusion | flops 570417152 | bytes 69271552 | tf_op jit(solution)/shard_map/qhd,khd->hqk/dot_general | solution.py:228
  642.8 52.8 %multiply_convert_fusion.1 = (bf16[8,512,1024]{2,1,0:T(8,128)(2,1)}, bf16[8,512,1024]{2,1,0:T(8,128)(2,1)S(1)}, bf16[8,512,1024]{2,1,0:T(8,128)(2,1)}, bf16[8,512,1024]{2,1,0:T(8,128)(2,1)}) fusion(f32[8,512,1024]{2,1,0:T(8,128)} %get-tuple-element.127, f32[8,512,1024]{2,1,0:T(8,128)} %get-tuple-element.115, f32[8,512]{1,0:T(8,128)S(1)} %get-tuple-element.44, ...), kind=kLoop, calls=%fused_computation.7 | loop fusion | flops 83886080 | bytes 168951808 | tf_op jit(solution)/shard_map/convert_element_type | solution.py:232
  695.7 8.3 fusion.103
  712.4 4.1 copy.43
  716.5 6.0 fusion.89
  722.6 6.2 fusion.90
  728.8 6.3 fusion.88
  741.1 5.6 convolution_bitcast_fusion.2
  746.8 6.9 convolution_bitcast_fusion
  753.7 6.1 pad_maximum_fusion
  761.4 14.9 fusion.142
  786.1 3.9 copy.57
  792.0 8.4 fusion.100
  800.4 266.5 %reduce-scatter.5.cloned.1.call-done = f32[4,128,1024]{1,2,0:T(8,128)} async-done(((f32[4,1024,1024]{1,2,0:T(8,128)}), f32[4,128,1024]{1,2,0:T(8,128)}) %reduce-scatter.5.cloned.1.call-update) | async-done | bytes 2097168 | tf_op jit(solution)/shard_map/reduce_scatter | solution.py:275
  1066.9 6.2 fusion.50
  1073.0 276.9 %reduce-scatter.9.cloned.1.call-done = f32[512,1024]{1,0:T(8,128)} async-done(((f32[4096,1024]{1,0:T(8,128)}), f32[512,1024]{1,0:T(8,128)}) %reduce-scatter.9.cloned.1.call-update) | async-done | bytes 2097168 | tf_op jit(solution)/shard_map/reduce_scatter | solution.py:187
  1349.9 7.8 fusion.99
  1357.8 12.9 fusion.47
  1370.7 4.0 copy.58
  1374.7 32.1 %reduce-scatter.11.cloned.1.call-done = f32[12,128]{1,0:T(8,128)} async-done(((f32[12,1024]{1,0:T(8,128)}), f32[12,128]{1,0:T(8,128)}) %reduce-scatter.11.cloned.1.call-update) | async-done | bytes 6160 | tf_op jit(solution)/shard_map/reduce_scatter | solution.py:276
  1408.8 5.8 psum.31
  1421.6 56.5 %all-reduce.3.cloned.1.call-done = (bf16[4,128,1024]{1,2,0:T(8,128)(2,1)}, bf16[128,4096]{1,0:T(8,128)(2,1)}, bf16[512,1024]{1,0:T(8,128)(2,1)}) async-done(((bf16[4,128,1024]{1,2,0:T(8,128)(2,1)}, bf16[128,4096]{1,0:T(8,128)(2,1)}, bf16[512,1024]{1,0:T(8,128)(2,1)}), (bf16[4,128,1024]{1,2,0:T(8,128)(2,1)}, bf16[128,4096]{1,0:T(8,128)(2,1)}, bf16[512,1024]{1,0:T(8,128)(2,1)})) %all-reduce.3.cloned.1.call-update) | async-done | bytes 3145744 | tf_op jit(solution)/shard_map/psum | solution.py:289
  1478.1 5.0 fusion.125
  1484.4 6.0 pad_maximum_fusion.2
  1490.4 6.7 copy.61
  1497.1 3.6 fusion.127
  1506.1 3.3 pad_maximum_fusion.4
  (322 shorter events, 109.5 us)
Async XLA Ops:
  7.2 384.7 %all-gather.3.cloned.1.call-start = ((), (), s32[]{:S(2)}) async-start(), calls=%async_computation.4 | async-start | bytes 9437184 | tf_op jit(solution)/shard_map/all_gather | solution.py:168
  10.0 430.2 %all-gather.5.cloned.1.call-start = ((), (), s32[]{:S(2)}) async-start(), calls=%async_computation.5 | async-start | bytes 9437184 | tf_op jit(solution)/shard_map/all_gather | solution.py:169
  13.2 132.5 %copy-start.24 = (f32[512,1024]{1,0:T(8,128)S(1)}, f32[512,1024]{1,0:T(8,128)}, u32[]{:S(2)}) copy-start(f32[512,1024]{1,0:T(8,128)} %param.30) | copy-start | bytes 6291460
  13.2 133.7 %copy-start.69 = (f32[12,128]{1,0:T(8,128)S(1)}, f32[12,128]{1,0:T(8,128)}, u32[]{:S(2)}) copy-start(f32[12,128]{1,0:T(8,128)} %param.34) | copy-start | bytes 18436
  13.2 198.3 %copy-start.87 = (s32[1,1024]{1,0:T(1,128)S(1)}, s32[1,1024]{1,0:T(1,128)}, u32[]{:S(2)}) copy-start(s32[1,1024]{1,0:T(1,128)} %param.21) | copy-start | bytes 12292
  17.1 199.5 %copy-start.37 = (bf16[1024,1024]{1,0:T(8,128)(2,1)S(1)}, bf16[1024,1024]{1,0:T(8,128)(2,1)}, u32[]{:S(2)}) copy-start(bf16[1024,1024]{1,0:T(8,128)(2,1)} %param.20) | copy-start | bytes 6291460
  17.1 59.1 %collective-permute-start = (bf16[4,128,1024]{1,2,0:T(8,128)(2,1)S(1)}, bf16[4,128,1024]{1,2,0:T(8,128)(2,1)S(1)}, u32[]{:S(2)}, u32[]{:S(2)}) collective-permute-start(bf16[4,128,1024]{1,2,0:T(8,128)(2,1)S(1)} %get-tuple-element.68), channel_id=1, source_target_pairs={{0,1},{1,2},{2,3},{3,4},{4,5},{5,6},{6,7},{7,0},{8,9},{9,10},{10,1... | collective-permute-start | bytes 3145736 | tf_op jit(solution)/shard_map/ppermute | solution.py:26
  20.1 58.6 %collective-permute-start.1 = (bf16[4,128,1024]{1,2,0:T(8,128)(2,1)S(1)}, bf16[4,128,1024]{1,2,0:T(8,128)(2,1)}, u32[]{:S(2)}, u32[]{:S(2)}) collective-permute-start(bf16[4,128,1024]{1,2,0:T(8,128)(2,1)S(1)} %get-tuple-element.68), channel_id=1, source_target_pairs={{0,7},{1,0},{2,1},{3,2},{4,3},{5,4},{6,5},{7,6},{8,15},{9,8},{10,9... | collective-permute-start | bytes 3145736 | tf_op jit(solution)/shard_map/ppermute | solution.py:31
  76.2 66.5 %collective-permute-start.2 = (bf16[4,128,1024]{1,2,0:T(8,128)(2,1)S(1)}, bf16[4,128,1024]{1,2,0:T(8,128)(2,1)}, u32[]{:S(2)}, u32[]{:S(2)}) collective-permute-start(bf16[4,128,1024]{1,2,0:T(8,128)(2,1)S(1)} %collective-permute-done), channel_id=1, source_target_pairs={{0,1},{1,2},{2,3},{3,4},{4,5},{5,6},{6,7},{7,0},{8,9},{9,10},{10,1... | collective-permute-start | bytes 3145736 | tf_op jit(solution)/shard_map/ppermute | solution.py:26
  78.7 133.6 %collective-permute-start.3 = (bf16[4,128,1024]{1,2,0:T(8,128)(2,1)}, bf16[4,128,1024]{1,2,0:T(8,128)(2,1)}, u32[]{:S(2)}, u32[]{:S(2)}) collective-permute-start(bf16[4,128,1024]{1,2,0:T(8,128)(2,1)} %collective-permute-done.1), channel_id=1, source_target_pairs={{0,7},{1,0},{2,1},{3,2},{4,3},{5,4},{6,5},{7,6},{8,15},{9,8},{10,9... | collective-permute-start | bytes 3145736 | tf_op jit(solution)/shard_map/ppermute | solution.py:31
  142.7 80.5 %collective-permute-start.4 = (bf16[4,128,1024]{1,2,0:T(8,128)(2,1)}, bf16[4,128,1024]{1,2,0:T(8,128)(2,1)}, u32[]{:S(2)}, u32[]{:S(2)}) collective-permute-start(bf16[4,128,1024]{1,2,0:T(8,128)(2,1)} %collective-permute-done.2), channel_id=1, source_target_pairs={{0,1},{1,2},{2,3},{3,4},{4,5},{5,6},{6,7},{7,0},{8,9},{9,10},{10,1... | collective-permute-start | bytes 3145736 | tf_op jit(solution)/shard_map/ppermute | solution.py:26
  146.9 645.1 %reduce-scatter.7.cloned.1.call-start = ((), (), s32[]{:S(2)}) async-start(), calls=%async_computation.7 | async-start | bytes 18874368 | tf_op jit(solution)/shard_map/reduce_scatter | solution.py:186
  212.2 125.7 %copy-start.10 = (pred[512,1024]{1,0:T(8,128)(4,1)}, pred[512,1024]{1,0:T(8,128)(4,1)S(1)}, u32[]{:S(2)}) copy-start(pred[512,1024]{1,0:T(8,128)(4,1)S(1)} %get-tuple-element.110) | copy-start | bytes 1572868
  212.2 164.1 %copy-start.12 = (pred[512,1024]{1,0:T(8,128)(4,1)}, pred[512,1024]{1,0:T(8,128)(4,1)S(1)}, u32[]{:S(2)}) copy-start(pred[512,1024]{1,0:T(8,128)(4,1)S(1)} %get-tuple-element.111) | copy-start | bytes 1572868
  212.3 38.1 %collective-permute-start.5 = (bf16[4,128,1024]{1,2,0:T(8,128)(2,1)}, bf16[4,128,1024]{1,2,0:T(8,128)(2,1)}, u32[]{:S(2)}, u32[]{:S(2)}) collective-permute-start(bf16[4,128,1024]{1,2,0:T(8,128)(2,1)} %collective-permute-done.3), channel_id=1, source_target_pairs={{0,7},{1,0},{2,1},{3,2},{4,3},{5,4},{6,5},{7,6},{8,15},{9,8},{10,9... | collective-permute-start | bytes 3145736 | tf_op jit(solution)/shard_map/ppermute | solution.py:31
  223.1 43.7 %collective-permute-start.6 = (bf16[4,128,1024]{1,2,0:T(8,128)(2,1)}, bf16[4,128,1024]{1,2,0:T(8,128)(2,1)S(1)}, u32[]{:S(2)}, u32[]{:S(2)}) collective-permute-start(bf16[4,128,1024]{1,2,0:T(8,128)(2,1)} %collective-permute-done.4), channel_id=1, source_target_pairs={{0,1},{1,2},{2,3},{3,4},{4,5},{5,6},{6,7},{7,0},{8,9},{9,10},{10,1... | collective-permute-start | bytes 3145736 | tf_op jit(solution)/shard_map/ppermute | solution.py:26
  229.9 38.1 %copy-start.38 = (bf16[1024,1024]{1,0:T(8,128)(2,1)S(1)}, bf16[1024,1024]{1,0:T(8,128)(2,1)}, u32[]{:S(2)}) copy-start(bf16[1024,1024]{1,0:T(8,128)(2,1)} %param.19) | copy-start | bytes 6291460
  281.9 65.3 %copy-start.4 = (bf16[1,1024,1024]{1,2,0:T(8,128)(2,1)}, bf16[1,1024,1024]{1,2,0:T(8,128)(2,1)S(1)}, u32[]{:S(2)}) copy-start(bf16[1,1024,1024]{1,2,0:T(8,128)(2,1)S(1)} %slice.220) | copy-start | bytes 6291460
  287.4 59.9 %copy-start.16 = (bf16[1,1024,16,64]{1,3,2,0:T(8,128)(2,1)}, bf16[1,1024,16,64]{1,3,2,0:T(8,128)(2,1)S(1)}, u32[]{:S(2)}) copy-start(bf16[1,1024,16,64]{1,3,2,0:T(8,128)(2,1)S(1)} %multiply_convert_fusion.5) | copy-start | bytes 6291460
  296.6 79.7 %copy-start.61 = (f32[8,512]{1,0:T(8,128)}, f32[8,512]{1,0:T(8,128)S(1)}, u32[]{:S(2)}) copy-start(f32[8,512]{1,0:T(8,128)S(1)} %get-tuple-element.114) | copy-start | bytes 49156
  305.0 32.9 %copy-start.63 = (f32[8,512]{1,0:T(8,128)}, f32[8,512]{1,0:T(8,128)S(1)}, u32[]{:S(2)}) copy-start(f32[8,512]{1,0:T(8,128)S(1)} %get-tuple-element.117) | copy-start | bytes 49156
  320.4 17.6 %copy-start.73 = (f32[8,512]{1,0:T(8,128)}, f32[8,512]{1,0:T(8,128)S(1)}, u32[]{:S(2)}) copy-start(f32[8,512]{1,0:T(8,128)S(1)} %get-tuple-element.48) | copy-start | bytes 49156
  320.4 10.7 copy-start
  347.2 21.7 %copy-start.18 = (bf16[1,1024,16,64]{1,3,2,0:T(8,128)(2,1)S(1)}, bf16[1,1024,16,64]{1,3,2,0:T(8,128)(2,1)}, u32[]{:S(2)}) copy-start(bf16[1,1024,16,64]{1,3,2,0:T(8,128)(2,1)} %add_convert_fusion.2) | copy-start | bytes 6291460
  360.7 15.7 %copy-start.75 = (f32[8,512]{1,0:T(8,128)}, f32[8,512]{1,0:T(8,128)S(1)}, u32[]{:S(2)}) copy-start(f32[8,512]{1,0:T(8,128)S(1)} %get-tuple-element.50) | copy-start | bytes 49156
  360.7 10.6 copy-start.1
  376.3 8.5 copy-start.34
  391.9 48.2 %copy-start.97 = (f32[1,1024]{1,0:T(1,128)S(1)}, f32[1,1024]{1,0:T(1,128)}, u32[]{:S(2)}) copy-start(f32[1,1024]{1,0:T(1,128)} %get-tuple-element.101) | copy-start | bytes 12292
  465.4 24.3 %copy-start.7 = (f32[1024,1024]{0,1:T(8,128)S(1)}, f32[1024,1024]{0,1:T(8,128)}, u32[]{:S(2)}) copy-start(f32[1024,1024]{0,1:T(8,128)} %copy-done.6) | copy-start | bytes 12582916
  504.8 562.1 %reduce-scatter.5.cloned.1.call-start = ((), (), s32[]{:S(2)}) async-start(), calls=%async_computation.6 | async-start | bytes 18874368 | tf_op jit(solution)/shard_map/reduce_scatter | solution.py:275
  509.1 52.8 %copy-start.53 = (f32[8,512]{1,0:T(8,128)}, f32[8,512]{1,0:T(8,128)S(1)}, u32[]{:S(2)}) copy-start(f32[8,512]{1,0:T(8,128)S(1)} %log_add_fusion.3) | copy-start | bytes 49156
  509.1 46.0 %copy-start.55 = (f32[8,512]{1,0:T(8,128)}, f32[8,512]{1,0:T(8,128)S(1)}, u32[]{:S(2)}) copy-start(f32[8,512]{1,0:T(8,128)S(1)} %log_add_fusion.2) | copy-start | bytes 49156
  509.2 36.0 %copy-start.57 = (f32[8,512]{1,0:T(8,128)}, f32[8,512]{1,0:T(8,128)S(1)}, u32[]{:S(2)}) copy-start(f32[8,512]{1,0:T(8,128)S(1)} %log_add_fusion.1) | copy-start | bytes 49156
  509.2 25.8 %copy-start.59 = (f32[8,512]{1,0:T(8,128)}, f32[8,512]{1,0:T(8,128)S(1)}, u32[]{:S(2)}) copy-start(f32[8,512]{1,0:T(8,128)S(1)} %log_add_fusion) | copy-start | bytes 49156
  535.0 10.1 copy-start.31
  535.1 20.1 %slice-start = ((s8[16777216]{0:T(1024)(128)(4,1)}), s8[4194304]{0:T(1024)(128)(4,1)S(1)}, s32[]{:S(2)}) async-start(s8[16777216]{0:T(1024)(128)(4,1)} %bitcast.261), calls=%async_computation.11 | async-start | bytes 8388608
  535.1 20.1 %slice-start.1 = ((s8[16777216]{0:T(1024)(128)(4,1)}), s8[4194304]{0:T(1024)(128)(4,1)S(1)}, s32[]{:S(2)}) async-start(s8[16777216]{0:T(1024)(128)(4,1)} %bitcast.261), calls=%async_computation.12 | async-start | bytes 8388608
  545.2 10.0 slice-start.2
  545.2 10.0 slice-start.3
  545.2 10.0 copy-start.11
  561.9 10.6 copy-start.26
  578.4 9.5 copy-start.20
  578.4 18.7 %slice-start.4 = ((s8[16777216]{0:T(1024)(128)(4,1)}), s8[4194304]{0:T(1024)(128)(4,1)S(1)}, s32[]{:S(2)}) async-start(s8[16777216]{0:T(1024)(128)(4,1)} %bitcast.263), calls=%async_computation.15 | async-start | bytes 8388608
  578.4 18.7 %slice-start.5 = ((s8[16777216]{0:T(1024)(128)(4,1)}), s8[4194304]{0:T(1024)(128)(4,1)S(1)}, s32[]{:S(2)}) async-start(s8[16777216]{0:T(1024)(128)(4,1)} %bitcast.263), calls=%async_computation.16 | async-start | bytes 8388608
  587.8 9.3 slice-start.6
  587.9 9.3 slice-start.7
  618.4 24.4 %copy-start.54 = (f32[8,512]{1,0:T(8,128)S(1)}, f32[8,512]{1,0:T(8,128)}, u32[]{:S(2)}) copy-start(f32[8,512]{1,0:T(8,128)} %copy-done.53) | copy-start | bytes 49156
  618.4 24.4 %copy-start.56 = (f32[8,512]{1,0:T(8,128)S(1)}, f32[8,512]{1,0:T(8,128)}, u32[]{:S(2)}) copy-start(f32[8,512]{1,0:T(8,128)} %copy-done.55) | copy-start | bytes 49156
  618.4 24.4 %copy-start.58 = (f32[8,512]{1,0:T(8,128)S(1)}, f32[8,512]{1,0:T(8,128)}, u32[]{:S(2)}) copy-start(f32[8,512]{1,0:T(8,128)} %copy-done.57) | copy-start | bytes 49156
  618.4 24.4 %copy-start.60 = (f32[8,512]{1,0:T(8,128)S(1)}, f32[8,512]{1,0:T(8,128)}, u32[]{:S(2)}) copy-start(f32[8,512]{1,0:T(8,128)} %copy-done.59) | copy-start | bytes 49156
  618.4 24.4 %copy-start.71 = (f32[8,512]{1,0:T(8,128)S(1)}, f32[8,512]{1,0:T(8,128)}, u32[]{:S(2)}) copy-start(f32[8,512]{1,0:T(8,128)} %get-tuple-element.46) | copy-start | bytes 49156
  618.4 24.4 %copy-start.72 = (f32[8,512]{1,0:T(8,128)S(1)}, f32[8,512]{1,0:T(8,128)}, u32[]{:S(2)}) copy-start(f32[8,512]{1,0:T(8,128)} %get-tuple-element.47) | copy-start | bytes 49156
  695.6 11.3 copy-start.2
  695.6 9.1 copy-start.3
  695.7 9.7 copy-start.17
  722.5 12.5 slice-start.10
  759.8 590.1 %reduce-scatter.9.cloned.1.call-start = ((), (), s32[]{:S(2)}) async-start(), calls=%async_computation.8 | async-start | bytes 18874368 | tf_op jit(solution)/shard_map/reduce_scatter | solution.py:187
  776.3 630.5 %reduce-scatter.11.cloned.1.call-start = ((), (), s32[]{:S(2)}) async-start(), calls=%async_computation.9 | async-start | bytes 73728 | tf_op jit(solution)/shard_map/reduce_scatter | solution.py:276
  791.5 275.4 %copy-start.15 = (f32[4,128,1024]{1,2,0:T(8,128)S(1)}, f32[4,128,1024]{1,2,0:T(8,128)}, u32[]{:S(2)}) copy-start(f32[4,128,1024]{1,2,0:T(8,128)} %copy-done.14) | copy-start | bytes 6291460
  791.5 686.6 %all-reduce.3.cloned.1.call-start = ((), (), s32[]{:S(2)}) async-start(), calls=%async_computation.10 | async-start | bytes 6291456 | tf_op jit(solution)/shard_map/psum | solution.py:289
  1370.7 36.1 %copy-start.70 = (f32[12,128]{1,0:T(8,128)S(1)}, f32[12,128]{1,0:T(8,128)}, u32[]{:S(2)}) copy-start(f32[12,128]{1,0:T(8,128)} %param.34) | copy-start | bytes 18436
  1370.7 36.2 %copy-start.93 = (f32[1,12,128]{2,0,1:T(1,128)S(1)}, f32[1,12,128]{2,0,1:T(1,128)}, u32[]{:S(2)}) copy-start(f32[1,12,128]{2,0,1:T(1,128)} %param.36) | copy-start | bytes 18436
  1370.7 36.1 %copy-start.94 = (f32[1,12,128]{2,0,1:T(1,128)S(1)}, f32[1,12,128]{2,0,1:T(1,128)}, u32[]{:S(2)}) copy-start(f32[1,12,128]{2,0,1:T(1,128)} %param.37) | copy-start | bytes 18436
  1370.7 43.9 %copy-start.92 = (f32[12,128]{1,0:T(8,128)S(1)}, f32[12,128]{1,0:T(8,128)}, u32[]{:S(2)}) copy-start(f32[12,128]{1,0:T(8,128)} %param.35) | copy-start | bytes 18436
  (61 other events, 276.5 us)
Sparse Core Ops, SparseCore 0:
  10.7 213.3 all-gather.2
  226.8 140.9 all-gather.4
  504.8 278.9 reduce-scatter.6
  787.5 279.3 reduce-scatter.4
  1070.5 279.3 reduce-scatter.8
  1352.9 53.9 reduce-scatter.10
  1410.5 67.4 all-reduce.2
